TPU v7x, 32 devices: a whole 2x2x4 slice. The times are simulated.
32 devices in a mesh: dp: 8 (over z, y), neg: 4 (over x, core).
Axes of the slice: x: 2, y: 2, z: 4, core: 2. Of those that a mesh axis runs over, the one named last changes fastest.
Arguments:
- user_embed: bfloat16 [24576, 256], P(('dp', 'neg')), may hold values from -25 to 25
- positive_embed: bfloat16 [24576, 256], P(('dp', 'neg')), may hold values from -6 to 6
- positive_ids: int32 [24576], P(('dp', 'neg')), may hold values from 0 to 1048575
- token_weights: int32 [24576], P(('dp', 'neg')), may hold values from 1 to 5
- offsets: int32 [8, 25], P('dp'), may hold values from 0 to 3072, as said below
- negative_embed: bfloat16 [32768, 256], P('neg'), may hold values from -6 to 6
- negative_ids: int32 [32768], P('neg'), may hold values from 0 to 1048575
Outputs:
- token_loss: float32 [24576], P(('dp', 'neg'))
- mean_loss: float32 [], replicated
Inputs may be any that keep to these rules, and one draw needn't show every extreme that they name: `offsets`: each row starts at 0 and does not fall; every user holds 2 or more slots; in every draw some group fills all 3072 slots.
All inputs are finite; a program needn't handle non-finite values.
Results may differ from a plain program's by a relative error of at most 0.0003.
Values may be sent and summed in bfloat16 or wider, within the bound.
No kernel may reach another device: no remote copies, remote signals or barrier semaphores. Data moves between devices by JAX's collectives and lax.ppermute only.
A program may use at most 64 MiB of HBM per device.

v0:
```python
import math
import jax
import jax.numpy as jnp
from jax import lax
from jax.sharding import PartitionSpec as P

floor_value = -1e30


def merged(value, axis, join):
    pieces = jax.tree.map(lambda part: lax.all_gather(part, axis), value)
    head = jax.tree.map(lambda part: part[0], pieces)
    tail = jax.tree.map(lambda part: part[1:], pieces)
    total, _ = lax.scan(lambda total, share: (join(total, share), None), head, tail)
    return total


def shard_partials(rows, row_ids, columns, column_ids, scale):
    logits = (
        lax.dot_general(rows, columns, (((1,), (1,)), ((), ())), preferred_element_type=jnp.float32)
        * scale
    )
    hit = row_ids[:, None] == column_ids[None, :]
    peak = jnp.max(jnp.where(hit, floor_value, logits), axis=1)
    summed = jnp.sum(jnp.where(hit, 0.0, jnp.exp(logits - peak[:, None])), axis=1)
    return (peak, summed)


def combine(first, second):
    peak = jnp.maximum(first[0], second[0])
    return (peak, first[1] * jnp.exp(first[0] - peak) + second[1] * jnp.exp(second[0] - peak))


def shards(
    user_embed, positive_embed, positive_ids, token_weights, offsets, negative_embed, negative_ids
):
    tok_rows = user_embed.shape[0]
    width = user_embed.shape[1]
    scale = 3.0 / math.sqrt(width)
    positions = lax.axis_index("neg") * tok_rows + jnp.arange(tok_rows, dtype=jnp.int32)
    ends = offsets[0, 1:]
    last_slot = jnp.any(positions[:, None] + 1 == ends[None, :], axis=1)
    live = (positions < offsets[0, -1]) & jnp.logical_not(last_slot)
    weight = token_weights.astype(jnp.float32)
    live_weight = weight * live.astype(jnp.float32)
    rows = lax.all_gather(user_embed, "neg", axis=0, tiled=True)
    row_ids = lax.all_gather(positive_ids, "neg", axis=0, tiled=True)
    number = rows.shape[0]
    block = math.gcd(number, 512)
    blocks = rows.reshape(number // block, block, width)
    id_blocks = row_ids.reshape(number // block, block)

    def one_block(pair):
        return shard_partials(pair[0], pair[1], negative_embed, negative_ids, scale)

    peaks, sums = lax.map(one_block, (blocks, id_blocks))
    new_peaks = peaks.reshape(number)
    new_sums = sums.reshape(number)
    peaks = new_peaks
    sums = new_sums
    peaks, sums = merged((peaks, sums), "neg", combine)
    own_start = lax.axis_index("neg") * tok_rows
    peaks = lax.dynamic_slice_in_dim(peaks, own_start, tok_rows, 0)
    sums = lax.dynamic_slice_in_dim(sums, own_start, tok_rows, 0)
    positive = (
        jnp.sum(user_embed.astype(jnp.float32) * positive_embed.astype(jnp.float32), axis=1) * scale
    )
    top = jnp.maximum(peaks, positive)
    lse = top + jnp.log(sums * jnp.exp(peaks - top) + jnp.exp(positive - top))
    token_loss = jnp.where(live, lse - positive, 0.0).astype(jnp.float32)
    weighted = jnp.sum(weight * token_loss)
    total, count = lax.psum((weighted, jnp.sum(live_weight)), ("dp", "neg"))
    return (token_loss, total / count)


def solution(mesh):
    in_specs = (
        P(("dp", "neg"), None),
        P(("dp", "neg"), None),
        P(("dp", "neg")),
        P(("dp", "neg")),
        P("dp", None),
        P("neg", None),
        P("neg"),
    )
    out_specs = (P(("dp", "neg")), P())
    return jax.shard_map(shards, mesh=mesh, in_specs=in_specs, out_specs=out_specs, check_vma=False)
```

profile of v0, /device:TPU:0, one launch (start us, length us, event | category | flops | bytes accessed | tf_op | source)
XLA Modules:
  0.0 153.4 jit_solution(13548246562837746475)
XLA Ops:
  7.2 0.7 all-gather.5.cloned.1.call-update
  7.9 0.7 reshape.22
  8.6 6.2 %all-gather = s32[4,1,768]{2,1,0:T(1,128)S(1)} all-gather(s32[1,1,768]{2,1,0:T(1,128)S(1)} %reshape.22), channel_id=1, replica_groups=mesh['dp'=8,'neg'=4] {'neg'}, dimensions={0}, use_global_device_ids=true | all-gather | bytes 15360 | tf_op jit(solution)/shard_map/all_gather | solution.py:47
  14.9 1.2 slice.18
  16.1 0.7 slice_bitcast_fusion
  16.9 1.3 multiply_reduce_fusion
  18.2 13.7 %all-gather.5.cloned.1.call-done = bf16[3072,256]{1,0:T(8,128)(2,1)} async-done(((bf16[768,256]{1,0:T(8,128)(2,1)}), bf16[3072,256]{1,0:T(8,128)(2,1)}) %all-gather.5.cloned.1.call-update) | async-done | bytes 1572880 | tf_op jit(solution)/shard_map/all_gather | solution.py:46
  31.9 59.9 %while.24 = (s32[]{:T(128)}, f32[6,512]{1,0:T(8,128)S(1)}, f32[6,512]{1,0:T(8,128)S(1)}, s32[6,512]{1,0:T(8,128)S(1)}, s32[8192]{0:T(1024)}, /*index=5*/bf16[6,5...) while((s32[]{:T(128)}, f32[6,512]{1,0:T(8,128)S(1)}, f32[6,512]{1,0:T(8,128)S(1)}, ...), condition=%wide.region_4.5_spmd, body=%wide.region_1.4_spmd.sunk | while | flops 2185231360 | bytes 38230660 | solution.py:56
  31.9 5.1 %fusion.16 = (f32[512]{0:T(512)S(1)}, f32[512,8192]{1,0:T(8,128)S(1)}) fusion(s32[8192]{0:T(1024)} %get-tuple-element.215, s32[512]{0:T(512)S(1)} %bitcast.44, bf16[8192,256]{1,0:T(8,128)(2,1)} %get-tuple-element.217, bf16[6,512,256]{2,1,0:T(8,128)(2,1)} %get-tuple-element.216, s32[]{:T(128)} %get-tuple-element.202), kind=kOutput, calls=%fused_computation.2.clone.1 | convolution fusion | flops 2164260352 | bytes 21271040 | tf_op jit(solution)/shard_map/while/body/eval_jaxpr/dot_general | solution.py:20
  37.1 4.6 %fusion.17 = f32[512]{0:T(512)S(1)} fusion(f32[512,8192]{1,0:T(8,128)S(1)} %get-tuple-element.183, f32[512]{0:T(512)S(1)} %get-tuple-element.182, s32[8192]{0:T(1024)S(1)} %copy-done, s32[512]{0:T(512)S(1)} %bitcast.45), kind=kLoop, calls=%fused_computation.3.clone.1 | loop fusion | flops 20971008 | bytes 16816128 | tf_op jit(solution)/shard_map/while/body/eval_jaxpr/reduce_sum | solution.py:25
  41.9 5.1 %fusion.16 = (f32[512]{0:T(512)S(1)}, f32[512,8192]{1,0:T(8,128)S(1)}) fusion(s32[8192]{0:T(1024)} %get-tuple-element.215, s32[512]{0:T(512)S(1)} %bitcast.44, bf16[8192,256]{1,0:T(8,128)(2,1)} %get-tuple-element.217, bf16[6,512,256]{2,1,0:T(8,128)(2,1)} %get-tuple-element.216, s32[]{:T(128)} %get-tuple-element.202), kind=kOutput, calls=%fused_computation.2.clone.1 | convolution fusion | flops 2164260352 | bytes 21271040 | tf_op jit(solution)/shard_map/while/body/eval_jaxpr/dot_general | solution.py:20
  47.1 4.6 %fusion.17 = f32[512]{0:T(512)S(1)} fusion(f32[512,8192]{1,0:T(8,128)S(1)} %get-tuple-element.183, f32[512]{0:T(512)S(1)} %get-tuple-element.182, s32[8192]{0:T(1024)S(1)} %copy-done, s32[512]{0:T(512)S(1)} %bitcast.45), kind=kLoop, calls=%fused_computation.3.clone.1 | loop fusion | flops 20971008 | bytes 16816128 | tf_op jit(solution)/shard_map/while/body/eval_jaxpr/reduce_sum | solution.py:25
  51.9 5.1 %fusion.16 = (f32[512]{0:T(512)S(1)}, f32[512,8192]{1,0:T(8,128)S(1)}) fusion(s32[8192]{0:T(1024)} %get-tuple-element.215, s32[512]{0:T(512)S(1)} %bitcast.44, bf16[8192,256]{1,0:T(8,128)(2,1)} %get-tuple-element.217, bf16[6,512,256]{2,1,0:T(8,128)(2,1)} %get-tuple-element.216, s32[]{:T(128)} %get-tuple-element.202), kind=kOutput, calls=%fused_computation.2.clone.1 | convolution fusion | flops 2164260352 | bytes 21271040 | tf_op jit(solution)/shard_map/while/body/eval_jaxpr/dot_general | solution.py:20
  57.1 4.6 %fusion.17 = f32[512]{0:T(512)S(1)} fusion(f32[512,8192]{1,0:T(8,128)S(1)} %get-tuple-element.183, f32[512]{0:T(512)S(1)} %get-tuple-element.182, s32[8192]{0:T(1024)S(1)} %copy-done, s32[512]{0:T(512)S(1)} %bitcast.45), kind=kLoop, calls=%fused_computation.3.clone.1 | loop fusion | flops 20971008 | bytes 16816128 | tf_op jit(solution)/shard_map/while/body/eval_jaxpr/reduce_sum | solution.py:25
  61.9 5.1 %fusion.16 = (f32[512]{0:T(512)S(1)}, f32[512,8192]{1,0:T(8,128)S(1)}) fusion(s32[8192]{0:T(1024)} %get-tuple-element.215, s32[512]{0:T(512)S(1)} %bitcast.44, bf16[8192,256]{1,0:T(8,128)(2,1)} %get-tuple-element.217, bf16[6,512,256]{2,1,0:T(8,128)(2,1)} %get-tuple-element.216, s32[]{:T(128)} %get-tuple-element.202), kind=kOutput, calls=%fused_computation.2.clone.1 | convolution fusion | flops 2164260352 | bytes 21271040 | tf_op jit(solution)/shard_map/while/body/eval_jaxpr/dot_general | solution.py:20
  67.1 4.6 %fusion.17 = f32[512]{0:T(512)S(1)} fusion(f32[512,8192]{1,0:T(8,128)S(1)} %get-tuple-element.183, f32[512]{0:T(512)S(1)} %get-tuple-element.182, s32[8192]{0:T(1024)S(1)} %copy-done, s32[512]{0:T(512)S(1)} %bitcast.45), kind=kLoop, calls=%fused_computation.3.clone.1 | loop fusion | flops 20971008 | bytes 16816128 | tf_op jit(solution)/shard_map/while/body/eval_jaxpr/reduce_sum | solution.py:25
  71.9 5.1 %fusion.16 = (f32[512]{0:T(512)S(1)}, f32[512,8192]{1,0:T(8,128)S(1)}) fusion(s32[8192]{0:T(1024)} %get-tuple-element.215, s32[512]{0:T(512)S(1)} %bitcast.44, bf16[8192,256]{1,0:T(8,128)(2,1)} %get-tuple-element.217, bf16[6,512,256]{2,1,0:T(8,128)(2,1)} %get-tuple-element.216, s32[]{:T(128)} %get-tuple-element.202), kind=kOutput, calls=%fused_computation.2.clone.1 | convolution fusion | flops 2164260352 | bytes 21271040 | tf_op jit(solution)/shard_map/while/body/eval_jaxpr/dot_general | solution.py:20
  77.0 4.6 %fusion.17 = f32[512]{0:T(512)S(1)} fusion(f32[512,8192]{1,0:T(8,128)S(1)} %get-tuple-element.183, f32[512]{0:T(512)S(1)} %get-tuple-element.182, s32[8192]{0:T(1024)S(1)} %copy-done, s32[512]{0:T(512)S(1)} %bitcast.45), kind=kLoop, calls=%fused_computation.3.clone.1 | loop fusion | flops 20971008 | bytes 16816128 | tf_op jit(solution)/shard_map/while/body/eval_jaxpr/reduce_sum | solution.py:25
  81.9 5.1 %fusion.16 = (f32[512]{0:T(512)S(1)}, f32[512,8192]{1,0:T(8,128)S(1)}) fusion(s32[8192]{0:T(1024)} %get-tuple-element.215, s32[512]{0:T(512)S(1)} %bitcast.44, bf16[8192,256]{1,0:T(8,128)(2,1)} %get-tuple-element.217, bf16[6,512,256]{2,1,0:T(8,128)(2,1)} %get-tuple-element.216, s32[]{:T(128)} %get-tuple-element.202), kind=kOutput, calls=%fused_computation.2.clone.1 | convolution fusion | flops 2164260352 | bytes 21271040 | tf_op jit(solution)/shard_map/while/body/eval_jaxpr/dot_general | solution.py:20
  87.0 4.6 %fusion.17 = f32[512]{0:T(512)S(1)} fusion(f32[512,8192]{1,0:T(8,128)S(1)} %get-tuple-element.183, f32[512]{0:T(512)S(1)} %get-tuple-element.182, s32[8192]{0:T(1024)S(1)} %copy-done, s32[512]{0:T(512)S(1)} %bitcast.45), kind=kLoop, calls=%fused_computation.3.clone.1 | loop fusion | flops 20971008 | bytes 16816128 | tf_op jit(solution)/shard_map/while/body/eval_jaxpr/reduce_sum | solution.py:25
  91.8 5.2 %all-gather.2 = f32[4,1,3072]{2,1,0:T(1,128)S(1)} all-gather(f32[1,1,3072]{2,1,0:T(1,128)S(1)} %reshape.26), channel_id=1, replica_groups=mesh['dp'=8,'neg'=4] {'neg'}, dimensions={0}, use_global_device_ids=true | all-gather | bytes 61440 | tf_op jit(solution)/shard_map/all_gather | solution.py:11
  97.1 5.2 %all-gather.1 = f32[4,1,3072]{2,1,0:T(1,128)S(1)} all-gather(f32[1,1,3072]{2,1,0:T(1,128)S(1)} %reshape.24), channel_id=1, replica_groups=mesh['dp'=8,'neg'=4] {'neg'}, dimensions={0}, use_global_device_ids=true | all-gather | bytes 61440 | tf_op jit(solution)/shard_map/all_gather | solution.py:11
  102.6 2.0 %select_reduce_fusion = (f32[]{:T(128)}, f32[]{:T(128)}, f32[768]{0:T(1024)}) fusion(s32[768]{0:T(1024)S(1)} %copy-done.1, pred[768]{0:T(1024)(128)(4,1)S(1)} %compare_reduce_fusion, s32[]{:T(128)} %bitcast.6, s32[]{:T(128)S(6)} %mul.31, f32[3072]{0:T(1024)S(1)} %get-tuple-element.71, s32[]{:T(128)S(6)} %select_n.15, f32[768]{0:T(1024)S(1)} %multiply_reduce_fusion, ...), kind=kLoop, calls=%fused_computation.16 | loop fusion | flops 13822 | bytes 16148 | tf_op jit(solution)/shard_map/reduce_sum | solution.py:72
  104.6 39.5 %all-reduce = (f32[]{:T(128)}, f32[]{:T(128)}) all-reduce(f32[]{:T(128)} %get-tuple-element.73, f32[]{:T(128)} %get-tuple-element.72), channel_id=1, replica_groups=mesh['dp'=8,'neg'=4] {'dp','neg'}, use_global_device_ids=true, to_apply=%region_9.10 | all-reduce | flops 2 | bytes 16 | tf_op jit(solution)/shard_map/psum | solution.py:72
  (54 shorter events, 1.4 us)
Async XLA Ops:
  7.2 24.8 %all-gather.5.cloned.1.call-start = ((), (), s32[]{:S(2)}) async-start(), calls=%async_computation | async-start | bytes 1966080 | tf_op jit(solution)/shard_map/all_gather | solution.py:46
  31.9 70.7 %copy-start.1 = (s32[768]{0:T(1024)S(1)}, s32[768]{0:T(1024)}, u32[]{:S(2)}) copy-start(s32[768]{0:T(1024)} %param.14) | copy-start | bytes 9220
  31.9 5.2 %copy-start = (s32[8192]{0:T(1024)S(1)}, s32[8192]{0:T(1024)}, u32[]{:S(2)}) copy-start(s32[8192]{0:T(1024)} %get-tuple-element.215) | copy-start | bytes 98308 | tf_op jit(solution)/shard_map/while
  41.9 5.2 %copy-start = (s32[8192]{0:T(1024)S(1)}, s32[8192]{0:T(1024)}, u32[]{:S(2)}) copy-start(s32[8192]{0:T(1024)} %get-tuple-element.215) | copy-start | bytes 98308 | tf_op jit(solution)/shard_map/while
  51.9 5.2 %copy-start = (s32[8192]{0:T(1024)S(1)}, s32[8192]{0:T(1024)}, u32[]{:S(2)}) copy-start(s32[8192]{0:T(1024)} %get-tuple-element.215) | copy-start | bytes 98308 | tf_op jit(solution)/shard_map/while
  61.9 5.2 %copy-start = (s32[8192]{0:T(1024)S(1)}, s32[8192]{0:T(1024)}, u32[]{:S(2)}) copy-start(s32[8192]{0:T(1024)} %get-tuple-element.215) | copy-start | bytes 98308 | tf_op jit(solution)/shard_map/while
  71.9 5.2 %copy-start = (s32[8192]{0:T(1024)S(1)}, s32[8192]{0:T(1024)}, u32[]{:S(2)}) copy-start(s32[8192]{0:T(1024)} %get-tuple-element.215) | copy-start | bytes 98308 | tf_op jit(solution)/shard_map/while
  81.8 5.2 %copy-start = (s32[8192]{0:T(1024)S(1)}, s32[8192]{0:T(1024)}, u32[]{:S(2)}) copy-start(s32[8192]{0:T(1024)} %get-tuple-element.215) | copy-start | bytes 98308 | tf_op jit(solution)/shard_map/while
Sparse Core Ops, SparseCore 0:
  9.5 22.3 all-gather.4
where the time goes:
time: 154 us; the launch traced here: 153 us
  blocking collectives  56.2 us (36%)
  other arithmetic  31.4 us (20%)
  matrix products  30.9 us (20%)
  between operations  16.6 us (11%)
  waiting for transfers between devices  14.4 us (9%)
  local copies, waits for them, and re-layouts  3.64 us (2%)
    psum x1, blocking collectives, shards(): total, count = lax.psum((weighted, jnp.sum(live_weight)), ('dp', 'neg'))  39.5 us
    dot_general x6, matrix products, shard_partials(): lax.dot_general(rows, columns, (((1,), (1,)), ((), ())), preferred_elemen...  30.9 us
    reduce_sum x6, other arithmetic, shard_partials(): jnp.sum(jnp.where(hit, 0.0, jnp.exp(logits - peak[:, None])), axis=1)  27.9 us
    all_gather x1, waiting for transfers between devices, shards(): rows = lax.all_gather(user_embed, 'neg', axis=0, tiled=True)  13.7 us
    all_gather x2, blocking collectives, merged(): pieces = jax.tree.map(lambda part: lax.all_gather(part, axis), value)  10.4 us
    all_gather x1, blocking collectives, shards(): row_ids = lax.all_gather(positive_ids, 'neg', axis=0, tiled=True)  6.2 us
  transfers between devices with their start and end apart: 1, of which 1 were waited for; matrix products, arithmetic and copies ran while one was open for 3% of the time, Pallas kernels for 0%

commit v1 on v0

--- a/solution.py
+++ b/solution.py
@@ -69,7 +69,7 @@
     lse = top + jnp.log(sums * jnp.exp(peaks - top) + jnp.exp(positive - top))
     token_loss = jnp.where(live, lse - positive, 0.0).astype(jnp.float32)
     weighted = jnp.sum(weight * token_loss)
-    total, count = lax.psum((weighted, jnp.sum(live_weight)), ("dp", "neg"))
+    total, count = lax.psum(lax.psum((weighted, jnp.sum(live_weight)), "dp"), "neg")
     return (token_loss, total / count)
 
 

time: 154 us -> 143 us (0.929)
  blocking collectives: 56.2 us -> 45.2 us
    psum x1 -> x2, blocking collectives: 39.5 us -> 28.6 us  [the longest x1 22.1 us: shards(): lax.psum((weighted, jnp.sum(live_weight)), 'dp')]
where the time goes in v1:
time: 143 us; the launch traced here: 142 us
  blocking collectives  45.2 us (32%)
  other arithmetic  31.3 us (22%)
  matrix products  30.9 us (22%)
  between operations  16.5 us (12%)
  waiting for transfers between devices  14.4 us (10%)
  local copies, waits for them, and re-layouts  3.64 us (3%)
    dot_general x6, matrix products, shard_partials(): lax.dot_general(rows, columns, (((1,), (1,)), ((), ())), preferred_elemen...  30.9 us
    reduce_sum x6, other arithmetic, shard_partials(): jnp.sum(jnp.where(hit, 0.0, jnp.exp(logits - peak[:, None])), axis=1)  27.9 us
    psum x1, blocking collectives, shards(): lax.psum((weighted, jnp.sum(live_weight)), 'dp')  22.1 us
    all_gather x1, waiting for transfers between devices, shards(): rows = lax.all_gather(user_embed, 'neg', axis=0, tiled=True)  13.7 us
    all_gather x2, blocking collectives, merged(): pieces = jax.tree.map(lambda part: lax.all_gather(part, axis), value)  10.4 us
    psum x1, blocking collectives, shards(): lax.psum(lax.psum((weighted, jnp.sum(live_weight)), 'dp'), 'neg')  6.54 us
    all_gather x1, blocking collectives, shards(): row_ids = lax.all_gather(positive_ids, 'neg', axis=0, tiled=True)  6.2 us
  transfers between devices with their start and end apart: 1, of which 1 were waited for; matrix products, arithmetic and copies ran while one was open for 3% of the time, Pallas kernels for 0%

profile of v1, /device:TPU:0, one launch (start us, length us, event | category | flops | bytes accessed | tf_op | source)
XLA Modules:
  0.0 142.4 jit_solution(8937993283505656552)
XLA Ops:
  7.9 0.7 reshape.22
  8.6 6.2 %all-gather = s32[4,1,768]{2,1,0:T(1,128)S(1)} all-gather(s32[1,1,768]{2,1,0:T(1,128)S(1)} %reshape.22), channel_id=1, replica_groups=mesh['dp'=8,'neg'=4] {'neg'}, dimensions={0}, use_global_device_ids=true | all-gather | bytes 15360 | tf_op jit(solution)/shard_map/all_gather | solution.py:47
  14.9 1.2 slice.18
  16.1 0.7 slice_bitcast_fusion
  16.9 1.3 multiply_reduce_fusion
  18.2 13.7 %all-gather.5.cloned.1.call-done = bf16[3072,256]{1,0:T(8,128)(2,1)} async-done(((bf16[768,256]{1,0:T(8,128)(2,1)}), bf16[3072,256]{1,0:T(8,128)(2,1)}) %all-gather.5.cloned.1.call-update) | async-done | bytes 1572880 | tf_op jit(solution)/shard_map/all_gather | solution.py:46
  31.9 59.9 %while.24 = (s32[]{:T(128)}, f32[6,512]{1,0:T(8,128)S(1)}, f32[6,512]{1,0:T(8,128)S(1)}, s32[6,512]{1,0:T(8,128)S(1)}, s32[8192]{0:T(1024)}, /*index=5*/bf16[6,5...) while((s32[]{:T(128)}, f32[6,512]{1,0:T(8,128)S(1)}, f32[6,512]{1,0:T(8,128)S(1)}, ...), condition=%wide.region_4.5_spmd, body=%wide.region_1.4_spmd.sunk | while | flops 2185231360 | bytes 38230660 | solution.py:56
  31.9 5.1 %fusion.16 = (f32[512]{0:T(512)S(1)}, f32[512,8192]{1,0:T(8,128)S(1)}) fusion(s32[8192]{0:T(1024)} %get-tuple-element.217, s32[512]{0:T(512)S(1)} %bitcast.44, bf16[8192,256]{1,0:T(8,128)(2,1)} %get-tuple-element.219, bf16[6,512,256]{2,1,0:T(8,128)(2,1)} %get-tuple-element.218, s32[]{:T(128)} %get-tuple-element.204), kind=kOutput, calls=%fused_computation.2.clone.1 | convolution fusion | flops 2164260352 | bytes 21271040 | tf_op jit(solution)/shard_map/while/body/eval_jaxpr/dot_general | solution.py:20
  37.1 4.6 %fusion.17 = f32[512]{0:T(512)S(1)} fusion(f32[512,8192]{1,0:T(8,128)S(1)} %get-tuple-element.185, f32[512]{0:T(512)S(1)} %get-tuple-element.184, s32[8192]{0:T(1024)S(1)} %copy-done, s32[512]{0:T(512)S(1)} %bitcast.45), kind=kLoop, calls=%fused_computation.3.clone.1 | loop fusion | flops 20971008 | bytes 16816128 | tf_op jit(solution)/shard_map/while/body/eval_jaxpr/reduce_sum | solution.py:25
  41.9 5.1 %fusion.16 = (f32[512]{0:T(512)S(1)}, f32[512,8192]{1,0:T(8,128)S(1)}) fusion(s32[8192]{0:T(1024)} %get-tuple-element.217, s32[512]{0:T(512)S(1)} %bitcast.44, bf16[8192,256]{1,0:T(8,128)(2,1)} %get-tuple-element.219, bf16[6,512,256]{2,1,0:T(8,128)(2,1)} %get-tuple-element.218, s32[]{:T(128)} %get-tuple-element.204), kind=kOutput, calls=%fused_computation.2.clone.1 | convolution fusion | flops 2164260352 | bytes 21271040 | tf_op jit(solution)/shard_map/while/body/eval_jaxpr/dot_general | solution.py:20
  47.1 4.6 %fusion.17 = f32[512]{0:T(512)S(1)} fusion(f32[512,8192]{1,0:T(8,128)S(1)} %get-tuple-element.185, f32[512]{0:T(512)S(1)} %get-tuple-element.184, s32[8192]{0:T(1024)S(1)} %copy-done, s32[512]{0:T(512)S(1)} %bitcast.45), kind=kLoop, calls=%fused_computation.3.clone.1 | loop fusion | flops 20971008 | bytes 16816128 | tf_op jit(solution)/shard_map/while/body/eval_jaxpr/reduce_sum | solution.py:25
  51.9 5.1 %fusion.16 = (f32[512]{0:T(512)S(1)}, f32[512,8192]{1,0:T(8,128)S(1)}) fusion(s32[8192]{0:T(1024)} %get-tuple-element.217, s32[512]{0:T(512)S(1)} %bitcast.44, bf16[8192,256]{1,0:T(8,128)(2,1)} %get-tuple-element.219, bf16[6,512,256]{2,1,0:T(8,128)(2,1)} %get-tuple-element.218, s32[]{:T(128)} %get-tuple-element.204), kind=kOutput, calls=%fused_computation.2.clone.1 | convolution fusion | flops 2164260352 | bytes 21271040 | tf_op jit(solution)/shard_map/while/body/eval_jaxpr/dot_general | solution.py:20
  57.1 4.6 %fusion.17 = f32[512]{0:T(512)S(1)} fusion(f32[512,8192]{1,0:T(8,128)S(1)} %get-tuple-element.185, f32[512]{0:T(512)S(1)} %get-tuple-element.184, s32[8192]{0:T(1024)S(1)} %copy-done, s32[512]{0:T(512)S(1)} %bitcast.45), kind=kLoop, calls=%fused_computation.3.clone.1 | loop fusion | flops 20971008 | bytes 16816128 | tf_op jit(solution)/shard_map/while/body/eval_jaxpr/reduce_sum | solution.py:25
  61.9 5.1 %fusion.16 = (f32[512]{0:T(512)S(1)}, f32[512,8192]{1,0:T(8,128)S(1)}) fusion(s32[8192]{0:T(1024)} %get-tuple-element.217, s32[512]{0:T(512)S(1)} %bitcast.44, bf16[8192,256]{1,0:T(8,128)(2,1)} %get-tuple-element.219, bf16[6,512,256]{2,1,0:T(8,128)(2,1)} %get-tuple-element.218, s32[]{:T(128)} %get-tuple-element.204), kind=kOutput, calls=%fused_computation.2.clone.1 | convolution fusion | flops 2164260352 | bytes 21271040 | tf_op jit(solution)/shard_map/while/body/eval_jaxpr/dot_general | solution.py:20
  67.1 4.6 %fusion.17 = f32[512]{0:T(512)S(1)} fusion(f32[512,8192]{1,0:T(8,128)S(1)} %get-tuple-element.185, f32[512]{0:T(512)S(1)} %get-tuple-element.184, s32[8192]{0:T(1024)S(1)} %copy-done, s32[512]{0:T(512)S(1)} %bitcast.45), kind=kLoop, calls=%fused_computation.3.clone.1 | loop fusion | flops 20971008 | bytes 16816128 | tf_op jit(solution)/shard_map/while/body/eval_jaxpr/reduce_sum | solution.py:25
  71.9 5.1 %fusion.16 = (f32[512]{0:T(512)S(1)}, f32[512,8192]{1,0:T(8,128)S(1)}) fusion(s32[8192]{0:T(1024)} %get-tuple-element.217, s32[512]{0:T(512)S(1)} %bitcast.44, bf16[8192,256]{1,0:T(8,128)(2,1)} %get-tuple-element.219, bf16[6,512,256]{2,1,0:T(8,128)(2,1)} %get-tuple-element.218, s32[]{:T(128)} %get-tuple-element.204), kind=kOutput, calls=%fused_computation.2.clone.1 | convolution fusion | flops 2164260352 | bytes 21271040 | tf_op jit(solution)/shard_map/while/body/eval_jaxpr/dot_general | solution.py:20
  77.0 4.6 %fusion.17 = f32[512]{0:T(512)S(1)} fusion(f32[512,8192]{1,0:T(8,128)S(1)} %get-tuple-element.185, f32[512]{0:T(512)S(1)} %get-tuple-element.184, s32[8192]{0:T(1024)S(1)} %copy-done, s32[512]{0:T(512)S(1)} %bitcast.45), kind=kLoop, calls=%fused_computation.3.clone.1 | loop fusion | flops 20971008 | bytes 16816128 | tf_op jit(solution)/shard_map/while/body/eval_jaxpr/reduce_sum | solution.py:25
  81.9 5.1 %fusion.16 = (f32[512]{0:T(512)S(1)}, f32[512,8192]{1,0:T(8,128)S(1)}) fusion(s32[8192]{0:T(1024)} %get-tuple-element.217, s32[512]{0:T(512)S(1)} %bitcast.44, bf16[8192,256]{1,0:T(8,128)(2,1)} %get-tuple-element.219, bf16[6,512,256]{2,1,0:T(8,128)(2,1)} %get-tuple-element.218, s32[]{:T(128)} %get-tuple-element.204), kind=kOutput, calls=%fused_computation.2.clone.1 | convolution fusion | flops 2164260352 | bytes 21271040 | tf_op jit(solution)/shard_map/while/body/eval_jaxpr/dot_general | solution.py:20
  87.0 4.6 %fusion.17 = f32[512]{0:T(512)S(1)} fusion(f32[512,8192]{1,0:T(8,128)S(1)} %get-tuple-element.185, f32[512]{0:T(512)S(1)} %get-tuple-element.184, s32[8192]{0:T(1024)S(1)} %copy-done, s32[512]{0:T(512)S(1)} %bitcast.45), kind=kLoop, calls=%fused_computation.3.clone.1 | loop fusion | flops 20971008 | bytes 16816128 | tf_op jit(solution)/shard_map/while/body/eval_jaxpr/reduce_sum | solution.py:25
  91.8 5.2 %all-gather.2 = f32[4,1,3072]{2,1,0:T(1,128)S(1)} all-gather(f32[1,1,3072]{2,1,0:T(1,128)S(1)} %reshape.26), channel_id=1, replica_groups=mesh['dp'=8,'neg'=4] {'neg'}, dimensions={0}, use_global_device_ids=true | all-gather | bytes 61440 | tf_op jit(solution)/shard_map/all_gather | solution.py:11
  97.1 5.2 %all-gather.1 = f32[4,1,3072]{2,1,0:T(1,128)S(1)} all-gather(f32[1,1,3072]{2,1,0:T(1,128)S(1)} %reshape.24), channel_id=1, replica_groups=mesh['dp'=8,'neg'=4] {'neg'}, dimensions={0}, use_global_device_ids=true | all-gather | bytes 61440 | tf_op jit(solution)/shard_map/all_gather | solution.py:11
  102.6 2.0 %select_reduce_fusion = (f32[]{:T(128)}, f32[]{:T(128)}, f32[768]{0:T(1024)}) fusion(s32[768]{0:T(1024)S(1)} %copy-done.1, pred[768]{0:T(1024)(128)(4,1)S(1)} %compare_reduce_fusion, s32[]{:T(128)} %bitcast.6, s32[]{:T(128)S(6)} %mul.31, f32[3072]{0:T(1024)S(1)} %get-tuple-element.71, s32[]{:T(128)S(6)} %select_n.15, f32[768]{0:T(1024)S(1)} %multiply_reduce_fusion, ...), kind=kLoop, calls=%fused_computation.16 | loop fusion | flops 13822 | bytes 16148 | tf_op jit(solution)/shard_map/reduce_sum | solution.py:72
  104.6 22.1 %all-reduce = (f32[]{:T(128)}, f32[]{:T(128)}) all-reduce(f32[]{:T(128)} %get-tuple-element.73, f32[]{:T(128)} %get-tuple-element.72), channel_id=1, replica_groups=mesh['dp'=8,'neg'=4] {'dp'}, use_global_device_ids=true, to_apply=%region_9.10 | all-reduce | flops 2 | bytes 16 | tf_op jit(solution)/shard_map/psum | solution.py:72
  126.6 6.5 %all-reduce.1 = (f32[]{:T(128)}, f32[]{:T(128)}) all-reduce(f32[]{:T(128)} %get-tuple-element.98, f32[]{:T(128)} %get-tuple-element.99), channel_id=1, replica_groups=mesh['dp'=8,'neg'=4] {'neg'}, use_global_device_ids=true, to_apply=%region_10.11 | all-reduce | flops 2 | bytes 16 | tf_op jit(solution)/shard_map/psum | solution.py:72
  (55 shorter events, 2.1 us)
Async XLA Ops:
  7.2 24.8 %all-gather.5.cloned.1.call-start = ((), (), s32[]{:S(2)}) async-start(), calls=%async_computation | async-start | bytes 1966080 | tf_op jit(solution)/shard_map/all_gather | solution.py:46
  31.9 70.7 %copy-start.1 = (s32[768]{0:T(1024)S(1)}, s32[768]{0:T(1024)}, u32[]{:S(2)}) copy-start(s32[768]{0:T(1024)} %param.14) | copy-start | bytes 9220
  31.9 5.2 %copy-start = (s32[8192]{0:T(1024)S(1)}, s32[8192]{0:T(1024)}, u32[]{:S(2)}) copy-start(s32[8192]{0:T(1024)} %get-tuple-element.217) | copy-start | bytes 98308 | tf_op jit(solution)/shard_map/while
  41.9 5.2 %copy-start = (s32[8192]{0:T(1024)S(1)}, s32[8192]{0:T(1024)}, u32[]{:S(2)}) copy-start(s32[8192]{0:T(1024)} %get-tuple-element.217) | copy-start | bytes 98308 | tf_op jit(solution)/shard_map/while
  51.9 5.2 %copy-start = (s32[8192]{0:T(1024)S(1)}, s32[8192]{0:T(1024)}, u32[]{:S(2)}) copy-start(s32[8192]{0:T(1024)} %get-tuple-element.217) | copy-start | bytes 98308 | tf_op jit(solution)/shard_map/while
  61.9 5.2 %copy-start = (s32[8192]{0:T(1024)S(1)}, s32[8192]{0:T(1024)}, u32[]{:S(2)}) copy-start(s32[8192]{0:T(1024)} %get-tuple-element.217) | copy-start | bytes 98308 | tf_op jit(solution)/shard_map/while
  71.9 5.2 %copy-start = (s32[8192]{0:T(1024)S(1)}, s32[8192]{0:T(1024)}, u32[]{:S(2)}) copy-start(s32[8192]{0:T(1024)} %get-tuple-element.217) | copy-start | bytes 98308 | tf_op jit(solution)/shard_map/while
  81.8 5.2 %copy-start = (s32[8192]{0:T(1024)S(1)}, s32[8192]{0:T(1024)}, u32[]{:S(2)}) copy-start(s32[8192]{0:T(1024)} %get-tuple-element.217) | copy-start | bytes 98308 | tf_op jit(solution)/shard_map/while
Sparse Core Ops, SparseCore 0:
  9.5 22.3 all-gather.4
